TPU v7x, 32 devices: a whole 2x2x4 slice. The times are simulated.
32 devices in a mesh: grp: 4 (over y, x), mem: 8 (over z, core).
Axes of the slice: x: 2, y: 2, z: 4, core: 2. Of those that a mesh axis runs over, the one named last changes fastest.
Arguments:
- params: float32 [4, 2048, 2048], P('grp', 'mem'), may hold values from -6 to 6
- estimate: float32 [4, 2048, 2048], P('grp', 'mem'), may hold values from -6 to 6
- mixed_sum: float32 [4, 2048, 2048], P('grp', 'mem'), may hold values from -6 to 6
- activations: bfloat16 [32768, 2048], P(('grp', 'mem')), may hold values from -6 to 6
- out_grads: bfloat16 [32768, 2048], P(('grp', 'mem')), may hold values from -6 to 6
- exponents: int32 [4, 32], P('grp', 'mem'), may hold values from 0 to 3
- edge_weight: float32 [4], replicated, may hold values from 0.1 to 0.45
Outputs:
- new_params: float32 [4, 2048, 2048], P('grp', 'mem')
- new_estimate: float32 [4, 2048, 2048], P('grp', 'mem')
- new_mixed: float32 [4, 2048, 2048], P('grp', 'mem')
All inputs are finite; a program needn't handle non-finite values.
Results may differ from a plain program's by a relative error of at most 0.01.
Values may be sent and summed in bfloat16 or wider, within the bound.
A program may use at most 128 MiB of HBM per device.

v0:
```python
import math

import jax
import jax.numpy as jnp
from jax import lax
from jax.sharding import PartitionSpec as P

step_size = 0.5
mixing_rate = 0.4


def shifted(value, axis, steps):
    count = lax.axis_size(axis)
    pairs = [(source, (source + steps) % count) for source in range(count)]
    return lax.ppermute(value, axis, pairs)


def on_device(params, estimate, mixed_sum, activations, out_grads, exponents, edge_weight):
    members = lax.axis_size("mem")
    groups = lax.axis_size("grp")
    shard_rows = params.shape[1]
    width = params.shape[2]
    local_rows = activations.shape[0]
    dims = (((0,), (0,)), ((), ()))
    full_term = lax.dot_general(activations, out_grads, dims, preferred_element_type=jnp.float32)
    gradient = lax.psum_scatter(
        full_term.astype(jnp.bfloat16), "mem", scatter_dimension=0, tiled=True
    ).astype(jnp.float32)
    factor = step_size / math.sqrt(members * local_rows)
    stepped = params - factor * gradient[None]
    change = stepped - estimate
    block_count = exponents.shape[1]
    scales = jnp.exp2(exponents.astype(jnp.float32))[:, :, None, None]
    blocked = change.reshape(1, block_count, shard_rows // block_count, width)
    levels = lax.optimization_barrier(jnp.clip(blocked / scales, -1.0, 1.0).astype(jnp.bfloat16))
    compressed = (
        (levels.astype(jnp.float32) * scales).astype(jnp.bfloat16).reshape(1, shard_rows, width)
    )
    left_piece = shifted(compressed, "grp", 1)
    right_piece = shifted(compressed, "grp", -1)
    own_piece = compressed.astype(jnp.float32)
    new_estimate = estimate + own_piece
    group_index = lax.axis_index("grp")
    weight_right = lax.dynamic_index_in_dim(edge_weight, group_index, 0, keepdims=False)
    weight_left = lax.dynamic_index_in_dim(
        edge_weight, (group_index + groups - 1) % groups, 0, keepdims=False
    )
    weight_self = 1.0 - weight_left - weight_right
    new_mixed = mixed_sum + weight_self * own_piece
    new_mixed = new_mixed + weight_left * left_piece.astype(jnp.float32)
    new_mixed = new_mixed + weight_right * right_piece.astype(jnp.float32)
    new_params = stepped + mixing_rate * (new_mixed - new_estimate)
    return (new_params, new_estimate, new_mixed)


def solution(mesh):
    in_specs = (
        P("grp", "mem", None),
        P("grp", "mem", None),
        P("grp", "mem", None),
        P(("grp", "mem"), None),
        P(("grp", "mem"), None),
        P("grp", "mem"),
        P(),
    )
    out_specs = (P("grp", "mem", None), P("grp", "mem", None), P("grp", "mem", None))
    return jax.shard_map(
        on_device, mesh=mesh, in_specs=in_specs, out_specs=out_specs, check_vma=False
    )
```

profile of v0, /device:TPU:8, one launch (start us, length us, event | category | flops | bytes accessed | tf_op | source)
XLA Modules:
  0.0 177.4 jit_solution(8745099668408099354)
XLA Ops:
  7.2 0.0 reduce-scatter.2.cloned.1.call-start
  7.2 14.1 %convolution_convert_fusion = bf16[2048,2048]{1,0:T(8,128)(2,1)} fusion(bf16[1024,2048]{1,0:T(8,128)(2,1)} %param.10, bf16[1024,2048]{1,0:T(8,128)(2,1)} %param.11), kind=kOutput, calls=%fused_computation | convolution fusion | flops 8594128896 | bytes 16777216 | tf_op jit(solution)/shard_map/dot_general | solution.py:25
  21.3 0.0 copy-start.3
  21.3 0.0 copy-start
  21.3 0.0 reduce-scatter.2.cloned.1.call-update
  21.3 0.6 copy-done.3
  22.0 87.4 %reduce-scatter.2.cloned.1.call-done = bf16[256,2048]{1,0:T(8,128)(2,1)} async-done(((bf16[2048,2048]{1,0:T(8,128)(2,1)}), bf16[256,2048]{1,0:T(8,128)(2,1)}) %reduce-scatter.2.cloned.1.call-update) | async-done | bytes 1048592 | tf_op jit(solution)/shard_map/reduce_scatter | solution.py:26
  109.4 0.0 copy-done
  109.4 2.3 %fusion.3 = f32[1,256,2048]{2,1,0:T(8,128)S(1)} fusion(f32[1,256,2048]{2,1,0:T(8,128)} %param.8, f32[1,256,2048]{2,1,0:T(8,128)S(1)} %copy-done, bf16[256,2048]{1,0:T(8,128)(2,1)} %reduce-scatter.2.cloned.1.call-done), kind=kLoop, calls=%fused_computation.10 | loop fusion | flops 2097152 | bytes 7340032 | tf_op jit(solution)/shard_map/sub | solution.py:31
  111.7 0.0 copy-start.2
  111.7 0.0 copy-start.1
  111.7 0.3 clamp_convert_fusion
  112.0 1.2 multiply_convert_fusion
  113.2 1.5 collective-permute-start
  114.7 1.4 collective-permute-start.1
  116.2 0.0 copy-done.2
  116.2 0.6 fusion.5
  118.0 22.1 %collective-permute-done = bf16[1,256,2048]{2,1,0:T(8,128)(2,1)} collective-permute-done((bf16[1,256,2048]{2,1,0:T(8,128)(2,1)}, bf16[1,256,2048]{2,1,0:T(8,128)(2,1)}, u32[]{:S(2)}, u32[]{:S(2)}) %collective-permute-start) | collective-permute-done | bytes 1048608 | tf_op jit(solution)/shard_map/ppermute | solution.py:15
  140.1 22.5 %collective-permute-done.1 = bf16[1,256,2048]{2,1,0:T(8,128)(2,1)} collective-permute-done((bf16[1,256,2048]{2,1,0:T(8,128)(2,1)}, bf16[1,256,2048]{2,1,0:T(8,128)(2,1)}, u32[]{:S(2)}, u32[]{:S(2)}) %collective-permute-start.1) | collective-permute-done | bytes 1048608 | tf_op jit(solution)/shard_map/ppermute | solution.py:15
  162.6 0.0 copy-done.1
  162.6 8.0 %multiply_add_fusion = (f32[1,256,2048]{2,1,0:T(8,128)}, f32[1,256,2048]{2,1,0:T(8,128)}, f32[1,256,2048]{2,1,0:T(8,128)}) fusion(f32[1,256,2048]{2,1,0:T(8,128)S(1)} %copy-done, bf16[256,2048]{1,0:T(8,128)(2,1)S(1)} %copy-done.1, f32[1,256,2048]{2,1,0:T(8,128)} %param.8, bf16[1,4,64,2048]{3,2,1,0:T(8,128)(2,1)} %multiply_convert_fusion, ...), kind=kLoop, calls=%fused_computation.7 | loop fusion | flops 8388608 | bytes 16777228 | tf_op jit(solution)/shard_map/add | solution.py:52
  (1 shorter events, 0.0 us)
Async XLA Ops:
  7.2 102.2 %reduce-scatter.2.cloned.1.call-start = ((), (), s32[]{:S(2)}) async-start(), calls=%async_computation.1 | async-start | bytes 9437184 | tf_op jit(solution)/shard_map/reduce_scatter | solution.py:26
  21.3 0.7 copy-start.3
  21.3 88.1 %copy-start = (f32[1,256,2048]{2,1,0:T(8,128)S(1)}, f32[1,256,2048]{2,1,0:T(8,128)}, u32[]{:S(2)}) copy-start(f32[1,256,2048]{2,1,0:T(8,128)} %param.7) | copy-start | bytes 6291460
  111.7 4.5 %copy-start.2 = (f32[4]{0:T(128)S(1)}, f32[4]{0:T(128)}, u32[]{:S(2)}) copy-start(f32[4]{0:T(128)} %param.13) | copy-start | bytes 52
  111.7 50.9 %copy-start.1 = (bf16[256,2048]{1,0:T(8,128)(2,1)S(1)}, bf16[256,2048]{1,0:T(8,128)(2,1)}, u32[]{:S(2)}) copy-start(bf16[256,2048]{1,0:T(8,128)(2,1)} %reduce-scatter.2.cloned.1.call-done) | copy-start | bytes 3145732
  113.2 26.8 %collective-permute-start = (bf16[1,256,2048]{2,1,0:T(8,128)(2,1)}, bf16[1,256,2048]{2,1,0:T(8,128)(2,1)}, u32[]{:S(2)}, u32[]{:S(2)}) collective-permute-start(bf16[1,256,2048]{2,1,0:T(8,128)(2,1)} %bitcast.5), channel_id=1, source_target_pairs={{0,8},{8,16},{16,24},{24,0},{1,9},{9,17},{17,25},{25,1},{2,10},{10... | collective-permute-start | bytes 3145736 | tf_op jit(solution)/shard_map/ppermute | solution.py:15
  114.7 47.8 %collective-permute-start.1 = (bf16[1,256,2048]{2,1,0:T(8,128)(2,1)}, bf16[1,256,2048]{2,1,0:T(8,128)(2,1)}, u32[]{:S(2)}, u32[]{:S(2)}) collective-permute-start(bf16[1,256,2048]{2,1,0:T(8,128)(2,1)} %bitcast.5), channel_id=1, source_target_pairs={{0,24},{8,0},{16,8},{24,16},{1,25},{9,1},{17,9},{25,17},{2,26},{10... | collective-permute-start | bytes 3145736 | tf_op jit(solution)/shard_map/ppermute | solution.py:15
Sparse Core Ops, SparseCore 0:
  21.5 87.8 reduce-scatter.1
where the time goes:
time: 179 us; the launch traced here: 177 us
  waiting for transfers between devices  132 us (74%)
  between operations  15.3 us (9%)
  matrix products  14.1 us (8%)
  other arithmetic  11.8 us (7%)
  starting transfers between devices  2.96 us (2%)
    reduce_scatter x1, waiting for transfers between devices, on_device(): lax.psum_scatter(full_term.astype(jnp.bfloat16), 'mem', scatter_dimension...  87.4 us
    ppermute x2, waiting for transfers between devices, shifted(): return lax.ppermute(value, axis, pairs)  44.6 us
    dot_general x1, matrix products, on_device(): lax.dot_general(activations, out_grads, dims, preferred_element_type=jnp....  14.1 us
    add x1, other arithmetic, on_device(): new_params = stepped + mixing_rate * (new_mixed - new_estimate)  7.99 us
  transfers between devices with their start and end apart: 3, of which 3 were waited for; matrix products, arithmetic and copies ran while one was open for 0% of the time, Pallas kernels for 0%

commit v1 on v0

v1 whole, which is shorter than its diff:
```python
import functools
import math

import jax
import jax.numpy as jnp
from jax import lax
from jax.experimental import pallas as pl
from jax.experimental.pallas import tpu as pltpu
from jax.sharding import PartitionSpec as P

step_size = 0.5
mixing_rate = 0.4
CHUNKS = 8
MESH = pl.DeviceIdType.MESH
f32 = jnp.float32
bf16 = jnp.bfloat16


def kernel(
    cfg,
    params, estimate, mixed, acts, grads, exponents, edges,
    out_params, out_estimate, out_mixed,
    act_v, act_t, grad_v, par_v, est_v, mix_v, new_p, new_e, new_m,
    mine, give, got, ring_out, ring_in, own, near, far,
    act_sem, grad_sem, par_sem, est_sem, mix_sem, put_sem,
    pair_s, pair_r, ring_s, ring_r, near_s, near_r, far_s, far_r,
):
    members, groups, chunks, rows, width, tokens, factor = cfg
    chips = members // 2
    hops = chips // 2
    cols = width // chunks
    half = rows // 2
    g = lax.axis_index("grp")
    m = lax.axis_index("mem")
    chip, core = m // 2, m % 2
    other = 1 - core
    sibling = chip * 2 + other
    ring_to = [
        lax.rem(chip + 1, chips) * 2 + core,
        lax.rem(chip + chips - 1, chips) * 2 + core,
    ]
    odd = g % 2
    partner = g + 1 - 2 * odd
    onward = lax.rem(g + 2 - 4 * odd + groups, groups)
    backward = lax.rem(g + groups - 2 + 4 * odd, groups)

    def act_copy(block):
        return pltpu.make_async_copy(
            acts.at[:, pl.ds(pl.multiple_of(block * rows, rows), rows)],
            act_v.at[block],
            act_sem.at[block],
        )

    def chunk_of(ref, j):
        return ref.at[:, pl.ds(pl.multiple_of(j * cols, cols), cols)]

    def grad_copy(j):
        return pltpu.make_async_copy(chunk_of(grads, j), grad_v.at[j], grad_sem.at[j])

    def load_copies(j):
        return [
            pltpu.make_async_copy(chunk_of(src.at[0], j), dst.at[j], sem.at[j])
            for src, dst, sem in (
                (params, par_v, par_sem), (estimate, est_v, est_sem), (mixed, mix_v, mix_sem)
            )
        ]

    def put_copy(which, j):
        src, dst = ((new_p, out_params), (new_e, out_estimate), (new_m, out_mixed))[which]
        return pltpu.make_async_copy(src.at[j], chunk_of(dst.at[0], j), put_sem.at[which, j])

    def pair_copy(j):
        return pltpu.make_async_remote_copy(
            src_ref=give.at[j], dst_ref=got.at[j],
            send_sem=pair_s.at[j], recv_sem=pair_r.at[j],
            device_id={"mem": sibling}, device_id_type=MESH,
        )

    def ring_copy(s, way, j):
        part = pl.ds(way * half, half) if s == 0 else pl.ds(0, rows)
        return pltpu.make_async_remote_copy(
            src_ref=ring_out.at[s, way, j, part],
            dst_ref=ring_in.at[s, way, j, part],
            send_sem=ring_s.at[s, way, j], recv_sem=ring_r.at[s, way, j],
            device_id={"mem": ring_to[way]}, device_id_type=MESH,
        )

    def near_copy(j):
        return pltpu.make_async_remote_copy(
            src_ref=own.at[j], dst_ref=near.at[j],
            send_sem=near_s.at[j], recv_sem=near_r.at[j],
            device_id={"grp": partner}, device_id_type=MESH,
        )

    def far_copy(j):
        return pltpu.make_async_remote_copy(
            src_ref=near.at[j], dst_ref=far.at[j],
            send_sem=far_s.at[j], recv_sem=far_r.at[j],
            device_id={"grp": onward}, device_id_type=MESH,
        )

    def blocks_of(parity):
        return lambda c: c * 2 + parity

    for c in range(chips):
        act_copy(c * 2 + other).start()
    grad_copy(0).start()
    for c in range(chips):
        act_copy(c * 2 + core).start()
    for j in range(1, chunks):
        grad_copy(j).start()
    for j in range(chunks):
        for copy in load_copies(j):
            copy.start()

    barrier = pltpu.get_barrier_semaphore()
    for peer in (
        {"mem": sibling}, {"mem": ring_to[0]}, {"mem": ring_to[1]},
        {"grp": partner}, {"grp": onward}, {"grp": backward},
    ):
        pl.semaphore_signal(barrier, inc=1, device_id=peer, device_id_type=MESH)
    pl.semaphore_wait(barrier, 6)

    def turn(parity):
        def body(c, carry):
            act_copy(c * 2 + parity).wait()
            start = pl.multiple_of(c * rows, rows)
            act_t[parity, pl.ds(start, rows), :] = act_v[c * 2 + parity].T
            return carry

        lax.fori_loop(0, chips, body, 0)

    def multiply(parity, j, into):
        into[j] = jnp.dot(act_t[parity], grad_v[j], preferred_element_type=f32).astype(bf16)

    def stage_multiply(j):
        @pl.when(j == 0)
        def _():
            turn(other)

        grad_copy(j).wait()
        multiply(other, j, give)
        pair_copy(j).start()

        @pl.when(j == 0)
        def _():
            turn(core)

        multiply(core, j, mine)

    def pair_sum(j, dest, start, count):
        at = pl.ds(pl.multiple_of(dest * rows + start, half), count)
        return mine[j, at, :].astype(f32) + got[j, at, :].astype(f32)

    def dest_of(s, way):
        ahead = hops - s
        return lax.rem(chip + (ahead if way == 0 else chips - ahead), chips)

    def stage_first(j):
        pair_copy(j).wait_recv()
        for way in (0, 1):
            ring_out[0, way, j, pl.ds(way * half, half), :] = pair_sum(
                j, dest_of(0, way), way * half, half
            ).astype(bf16)
            ring_copy(0, way, j).start()

    def stage_ring(s, j):
        for way in (0, 1):
            ring_copy(s - 1, way, j).wait_recv()
            for part in (0, 1):
                total = pair_sum(j, dest_of(s, way), part * half, half)
                if s >= 2 or part == way:
                    total = total + ring_in[s - 1, way, j, pl.ds(part * half, half), :].astype(f32)
                ring_out[s, way, j, pl.ds(part * half, half), :] = total.astype(bf16)
            ring_copy(s, way, j).start()

    weight_right = edges[g]
    weight_left = edges[lax.rem(g + groups - 1, groups)]
    weight_self = 1.0 - weight_left - weight_right
    weight_near = jnp.where(odd == 1, weight_left, weight_right)
    weight_far = jnp.where(odd == 1, weight_right, weight_left)
    blocks = exponents.shape[1]
    block_rows = rows // blocks

    def stage_compress(j):
        for way in (0, 1):
            ring_copy(hops - 1, way, j).wait_recv()
        for copy in load_copies(j):
            copy.wait()
        for b in range(blocks):
            exponent = exponents[0, b]
            scale = (jnp.int32(1) << exponent).astype(f32)
            inverse = (jnp.int32(1) << (15 - exponent)).astype(f32) * (2.0 ** -15)
            at = pl.ds(b * block_rows, block_rows)
            here = pl.ds(pl.multiple_of(chip * rows + b * block_rows, block_rows), block_rows)
            gradient = (
                mine[j, here, :].astype(f32)
                + got[j, here, :].astype(f32)
                + ring_in[hops - 1, 0, j, at, :].astype(f32)
                + ring_in[hops - 1, 1, j, at, :].astype(f32)
            )
            stepped = par_v[j, at, :] - factor * gradient
            base = est_v[j, at, :]
            levels = jnp.clip((stepped - base) * inverse, -1.0, 1.0).astype(bf16)
            compressed = levels.astype(f32) * scale
            own[j, at, :] = compressed.astype(bf16)
            new_p[j, at, :] = stepped
            new_e[j, at, :] = base + compressed
            new_m[j, at, :] = mix_v[j, at, :] + weight_self * compressed
        near_copy(j).start()
        put_copy(1, j).start()

    def stage_forward(j):
        near_copy(j).wait_recv()
        far_copy(j).start()

    def stage_finish(j):
        far_copy(j).wait_recv()
        total = (
            new_m[j] + weight_near * near[j].astype(f32) + weight_far * far[j].astype(f32)
        )
        new_m[j] = total
        new_p[j] = new_p[j] + mixing_rate * (total - new_e[j])
        put_copy(2, j).start()
        put_copy(0, j).start()

    stages = [(stage_multiply, 0), (stage_first, 1)]
    for s in range(1, hops):
        stages.append((functools.partial(stage_ring, s), 1 + s))
    stages += [(stage_compress, 1 + hops), (stage_forward, 2 + hops), (stage_finish, 3 + hops)]
    order = stages[1:] + stages[:1]

    def body(t, carry):
        for stage, lag in order:
            j = t - lag

            @pl.when(jnp.logical_and(j >= 0, j < chunks))
            def _(stage=stage, j=j):
                stage(j)

        return carry

    lax.fori_loop(0, chunks + 3 + hops, body, 0)

    def drain(j, carry):
        pair_copy(j).wait_send()
        for s in range(hops):
            for way in (0, 1):
                ring_copy(s, way, j).wait_send()
        near_copy(j).wait_send()
        far_copy(j).wait_send()
        for which in range(3):
            put_copy(which, j).wait()
        return carry

    lax.fori_loop(0, chunks, drain, 0)


def on_device(members, groups, params, estimate, mixed, acts, grads, exponents, edges):
    rows, width = params.shape[1:]
    tokens = acts.shape[0]
    chunks = CHUNKS
    cols = width // chunks
    chips = members // 2
    hops = chips // 2
    factor = step_size / math.sqrt(members * tokens)
    cfg = (members, groups, chunks, rows, width, tokens, factor)
    wide = (chunks, rows, cols)
    tall = (chunks, chips * rows, cols)
    dma = pltpu.SemaphoreType.DMA
    any_spec = pl.BlockSpec(memory_space=pl.ANY)
    smem = pl.BlockSpec(memory_space=pltpu.SMEM)
    return pl.pallas_call(
        functools.partial(kernel, cfg),
        out_shape=[jax.ShapeDtypeStruct(params.shape, f32)] * 3,
        in_specs=[any_spec] * 5 + [smem] * 2,
        out_specs=[any_spec] * 3,
        scratch_shapes=[
            pltpu.VMEM((members, tokens, rows), bf16),
            pltpu.VMEM((2, chips * rows, tokens), bf16),
            pltpu.VMEM((chunks, tokens, cols), bf16),
            *[pltpu.VMEM(wide, f32)] * 6,
            *[pltpu.VMEM(tall, bf16)] * 3,
            *[pltpu.VMEM((hops, 2) + wide, bf16)] * 2,
            *[pltpu.VMEM(wide, bf16)] * 3,
            dma((members,)), dma((chunks,)), dma((chunks,)), dma((chunks,)), dma((chunks,)),
            dma((3, chunks)),
            dma((chunks,)), dma((chunks,)),
            dma((hops, 2, chunks)), dma((hops, 2, chunks)),
            dma((chunks,)), dma((chunks,)), dma((chunks,)), dma((chunks,)),
        ],
        compiler_params=pltpu.CompilerParams(
            collective_id=0, has_side_effects=True, vmem_limit_bytes=66 * 1000 * 1000
        ),
    )(params, estimate, mixed, acts, grads, exponents, edges)


def solution(mesh):
    shard = P("grp", "mem", None)
    tokens = P(("grp", "mem"), None)
    return jax.shard_map(
        functools.partial(on_device, mesh.shape["mem"], mesh.shape["grp"]),
        mesh=mesh,
        in_specs=(shard, shard, shard, tokens, tokens, P("grp", "mem"), P()),
        out_specs=(shard, shard, shard),
        check_vma=False,
    )
```

time: 179 us -> 99.2 us (0.55)
  waiting for transfers between devices: 132 us -> 0 us
  Pallas kernels: 0 us -> 89.9 us
  between operations: 15.3 us -> 0.65 us
  matrix products: 14.1 us -> 0 us
  other arithmetic: 11.8 us -> 0 us
  local copies, waits for them, and re-layouts: 1.25 us -> 6.95 us
  starting transfers between devices: 2.96 us -> 0 us
    pallas_call x0 -> x1, Pallas kernels: none -> 89.9 us  [on_device(): pl.pallas_call(functools.partial(kernel, cfg), out_shape=[jax.ShapeDtypeS...]
    reduce_scatter x1 -> x0, waiting for transfers between devices: 87.4 us -> none  [on_device(): lax.psum_scatter(full_term.astype(jnp.bfloat16), 'mem', scatter_dimension...]
    ppermute x2 -> x0, waiting for transfers between devices: 44.6 us -> none  [shifted(): return lax.ppermute(value, axis, pairs)]
    dot_general x1 -> x0, matrix products: 14.1 us -> none  [on_device(): lax.dot_general(activations, out_grads, dims, preferred_element_type=jnp....]
    add x1 -> x0, other arithmetic: 7.99 us -> none  [on_device(): new_params = stepped + mixing_rate * (new_mixed - new_estimate)]
    unnamed x8 -> x7, local copies, waits for them, and re-layouts: 0.64 us -> 6.95 us
    ppermute x2 -> x0, starting transfers between devices: 2.92 us -> none  [shifted(): return lax.ppermute(value, axis, pairs)]
    sub x1 -> x0, other arithmetic: 2.3 us -> none  [on_device(): change = stepped - estimate]
  transfers between devices with their start and end apart: 3 -> 0, of which waited for: 3 -> 0; matrix products, arithmetic and copies ran while one was open for 0% -> 0% of each run, Pallas kernels for 0% -> 0%
where the time goes in v1:
time: 99.2 us; the launch traced here: 97.5 us
  Pallas kernels  89.9 us (91%)
  local copies, waits for them, and re-layouts  6.95 us (7%)
    pallas_call x1, Pallas kernels, on_device(): pl.pallas_call(functools.partial(kernel, cfg), out_shape=[jax.ShapeDtypeS...  89.9 us
    unnamed x7, local copies, waits for them, and re-layouts  6.95 us

profile of v1, /device:TPU:8, one launch (start us, length us, event | category | flops | bytes accessed | tf_op | source)
XLA Modules:
  0.0 97.5 jit_solution(11050653515372676559)
XLA Ops:
  0.6 89.9 %shard_map.94 = (f32[1,256,2048]{2,1,0:T(8,128)}, f32[1,256,2048]{2,1,0:T(8,128)}, f32[1,256,2048]{2,1,0:T(8,128)}) custom-call(f32[1,256,2048]{2,1,0:T(8,128)} %params.1, f32[1,256,2048]{2,1,0:T(8,128)} %estimate.1, f32[1,256,2048]{2,1,0:T(8,128)} %mixed.1, bf16[1024,2048]{1,0:T(8,128)(2,1)} %acts.1, bf16[1024,2048]{1,0:T(8,128)(2,1)} %grads.1, ...), custom_call_target="tpu_custom_call" | custom-call | tf_op jit(solution)/shard_map/pallas_call | solution.py:273
  90.6 0.0 copy-start.1
  90.6 3.3 %copy.13 = f32[1,256,2048]{2,1,0:T(8,128)} copy(f32[1,256,2048]{2,1,0:T(8,128)} %get-tuple-element.6) | data formatting | bytes 4194304
  93.9 0.0 copy-done.1
  93.9 0.0 copy-start
  93.9 1.3 %copy.14 = f32[1,256,2048]{2,1,0:T(8,128)} copy(f32[1,256,2048]{2,1,0:T(8,128)S(1)} %copy-done.1) | data formatting | bytes 4194304
  95.2 1.0 %copy-done = f32[1,256,2048]{2,1,0:T(8,128)S(1)} copy-done((f32[1,256,2048]{2,1,0:T(8,128)S(1)}, f32[1,256,2048]{2,1,0:T(8,128)}, u32[]{:S(2)}) %copy-start) | copy-done | bytes 2097176
  96.2 1.3 %copy.15 = f32[1,256,2048]{2,1,0:T(8,128)} copy(f32[1,256,2048]{2,1,0:T(8,128)S(1)} %copy-done) | data formatting | bytes 4194304
Async XLA Ops:
  90.6 3.3 %copy-start.1 = (f32[1,256,2048]{2,1,0:T(8,128)S(1)}, f32[1,256,2048]{2,1,0:T(8,128)}, u32[]{:S(2)}) copy-start(f32[1,256,2048]{2,1,0:T(8,128)} %get-tuple-element.7) | copy-start | bytes 6291460
  93.9 2.3 %copy-start = (f32[1,256,2048]{2,1,0:T(8,128)S(1)}, f32[1,256,2048]{2,1,0:T(8,128)}, u32[]{:S(2)}) copy-start(f32[1,256,2048]{2,1,0:T(8,128)} %get-tuple-element.8) | copy-start | bytes 6291460

commit v2 on v1

v2 whole, which is shorter than its diff:
```python
import functools
import math

import jax
import jax.numpy as jnp
from jax import lax
from jax.experimental import pallas as pl
from jax.experimental.pallas import tpu as pltpu
from jax.sharding import PartitionSpec as P

step_size = 0.5
mixing_rate = 0.4
CHUNKS = 8
DEPTH = 3
LAG = 2
MESH = pl.DeviceIdType.MESH
f32 = jnp.float32
bf16 = jnp.bfloat16


def kernel(
    cfg,
    params, estimate, mixed, acts, grads, exponents, edges,
    out_params, out_estimate, out_mixed,
    act_v, act_t, grad_v, par_v, est_v, mix_v,
    mine, give, got, line_out, line_in, own, near, far,
    act_sem, grad_sem, par_sem, est_sem, mix_sem,
    pair_s, pair_r, line_s, line_r, near_s, near_r, far_s, far_r,
):
    members, groups, chunks, rows, width, tokens, factor = cfg
    chips = members // 2
    pairs = chips // 2
    items = pairs * chunks
    slots = (chips - 1) * chunks
    cols = width // chunks
    g = lax.axis_index("grp")
    m = lax.axis_index("mem")
    chip, core = m // 2, m % 2
    other = 1 - core
    sibling = chip * 2 + other
    line_to = [
        lax.rem(chip + 1, chips) * 2 + core,
        lax.rem(chip + chips - 1, chips) * 2 + core,
    ]
    place = [chip, chips - 1 - chip]
    odd = g % 2
    partner = g + 1 - 2 * odd
    onward = lax.rem(g + 2 - 4 * odd + groups, groups)
    backward = lax.rem(g + groups - 2 + 4 * odd, groups)

    def act_copy(block):
        return pltpu.make_async_copy(
            acts.at[:, pl.ds(pl.multiple_of(block * rows, rows), rows)],
            act_v.at[block],
            act_sem.at[block],
        )

    def chunk_of(ref, j):
        return ref.at[:, pl.ds(pl.multiple_of(j * cols, cols), cols)]

    def grad_copy(j):
        return pltpu.make_async_copy(chunk_of(grads, j), grad_v.at[j], grad_sem.at[j])

    def load_copies(j):
        return [
            pltpu.make_async_copy(chunk_of(src.at[0], j), dst.at[j], sem.at[j])
            for src, dst, sem in (
                (params, par_v, par_sem), (estimate, est_v, est_sem), (mixed, mix_v, mix_sem)
            )
        ]

    def lanes(j):
        return pl.ds(pl.multiple_of(j * cols, cols), cols)

    def pair_copy(i):
        return pltpu.make_async_remote_copy(
            src_ref=give.at[i], dst_ref=got.at[i],
            send_sem=pair_s.at[i], recv_sem=pair_r.at[i],
            device_id={"mem": sibling}, device_id_type=MESH,
        )

    def line_copy(way, slot):
        return pltpu.make_async_remote_copy(
            src_ref=line_out.at[way, slot], dst_ref=line_in.at[way, slot],
            send_sem=line_s.at[way, slot], recv_sem=line_r.at[way, slot],
            device_id={"mem": line_to[way]}, device_id_type=MESH,
        )

    def near_copy(j):
        return pltpu.make_async_remote_copy(
            src_ref=own.at[j], dst_ref=near.at[j],
            send_sem=near_s.at[j], recv_sem=near_r.at[j],
            device_id={"grp": partner}, device_id_type=MESH,
        )

    def far_copy(j):
        return pltpu.make_async_remote_copy(
            src_ref=near.at[j], dst_ref=far.at[j],
            send_sem=far_s.at[j], recv_sem=far_r.at[j],
            device_id={"grp": onward}, device_id_type=MESH,
        )

    def members_of(b):
        return [(b, other), (chips - 1 - b, other), (b, core), (chips - 1 - b, core)]

    barrier = pltpu.get_barrier_semaphore()
    for peer in (
        {"mem": sibling}, {"mem": line_to[0]}, {"mem": line_to[1]},
        {"grp": partner}, {"grp": onward}, {"grp": backward},
    ):
        pl.semaphore_signal(barrier, inc=1, device_id=peer, device_id_type=MESH)

    grad_copy(0).start()
    for b in range(pairs):
        for dest, parity in members_of(b):
            act_copy(dest * 2 + parity).start()
        if b == 0:
            for j in range(1, chunks):
                grad_copy(j).start()
    for j in range(chunks):
        for copy in load_copies(j):
            copy.start()

    def multiply(i, before_send):
        b, j = i // chunks, i % chunks

        @pl.when(b == 0)
        def _():
            grad_copy(j).wait()

        def turn(dest, parity):
            @pl.when(j == 0)
            def _():
                block = dest * 2 + parity
                act_copy(block).wait()
                act_t[block] = act_v[block].T

        def product(dest, parity):
            return jnp.dot(
                act_t[dest * 2 + parity], grad_v[j], preferred_element_type=f32
            ).astype(bf16)

        for which, dest in ((0, b), (1, chips - 1 - b)):
            turn(dest, other)
            give[i, which] = product(dest, other)
        before_send()
        pair_copy(i).start()
        for which, dest in ((0, b), (1, chips - 1 - b)):
            turn(dest, core)
            mine[i, which] = product(dest, core)

    def pair_sum(i, which):
        return mine[i, which].astype(f32) + got[i, which].astype(f32)

    def pass_on(way, t):
        slot = t - LAG * place[way]
        block = slot // chunks
        j = slot % chunks

        @pl.when(jnp.logical_and(slot >= 0, slot < (chips - 1 - place[way]) * chunks))
        def _():
            @pl.when(slot >= DEPTH)
            def _():
                line_copy(way, slot - DEPTH).wait_send()

            late = block >= pairs
            i = jnp.where(late, chips - 1 - block, block) * chunks + j
            which = jnp.where(late, way, 1 - way)

            @pl.when(place[way] == 0)
            def _():
                line_out[way, slot] = pair_sum(i, which).astype(bf16)

            @pl.when(place[way] > 0)
            def _():
                line_copy(way, slot).wait_recv()
                line_out[way, slot] = (
                    pair_sum(i, which) + line_in[way, slot].astype(f32)
                ).astype(bf16)

            line_copy(way, slot).start()

    weight_right = edges[g]
    weight_left = edges[lax.rem(g + groups - 1, groups)]
    weight_self = 1.0 - weight_left - weight_right
    weight_near = jnp.where(odd == 1, weight_left, weight_right)
    weight_far = jnp.where(odd == 1, weight_right, weight_left)
    blocks = exponents.shape[1]
    block_rows = rows // blocks
    first = jnp.int32(0)
    for c in range(chips):
        after = [(chips - 1 - c) * chunks + LAG * c] if c > 0 else []
        if c < chips - 1:
            after.append(c * chunks + LAG * (chips - 1 - c))
        first = jnp.where(chip == c, max(after), first)
    own_which = jnp.where(chip >= pairs, 1, 0)
    own_block = jnp.where(chip >= pairs, chips - 1 - chip, chip)

    def compress(j):
        slot_of = [(chips - 1 - place[way]) * chunks + j for way in (0, 1)]
        for way in (0, 1):
            @pl.when(place[way] > 0)
            def _(way=way):
                line_copy(way, slot_of[way]).wait_recv()

            @pl.when(place[way] == 0)
            def _(way=way):
                line_in[way, slot_of[way]] = jnp.zeros((rows, cols), bf16)

        for copy in load_copies(j):
            copy.wait()
        i = own_block * chunks + j
        for b in range(blocks):
            exponent = exponents[0, b]
            scale = (jnp.int32(1) << exponent).astype(f32)
            inverse = (jnp.int32(1) << (15 - exponent)).astype(f32) * (2.0 ** -15)
            at = pl.ds(b * block_rows, block_rows)
            gradient = (
                mine[i, own_which, at, :].astype(f32)
                + got[i, own_which, at, :].astype(f32)
                + line_in[0, slot_of[0], at, :].astype(f32)
                + line_in[1, slot_of[1], at, :].astype(f32)
            )
            stepped = par_v[j, at, :] - factor * gradient
            base = est_v[j, at, :]
            levels = jnp.clip((stepped - base) * inverse, -1.0, 1.0).astype(bf16)
            compressed = levels.astype(f32) * scale
            own[j, at, :] = compressed.astype(bf16)
            out_params[0, at, lanes(j)] = stepped
            out_estimate[0, at, lanes(j)] = base + compressed
            out_mixed[0, at, lanes(j)] = mix_v[j, at, :] + weight_self * compressed
        near_copy(j).start()

    def forward(j):
        near_copy(j).wait_recv()
        far_copy(j).start()

    def finish(j):
        far_copy(j).wait_recv()
        total = (
            out_mixed[0, :, lanes(j)] + weight_near * near[j].astype(f32) + weight_far * far[j].astype(f32)
        )
        out_mixed[0, :, lanes(j)] = total
        out_params[0, :, lanes(j)] = out_params[0, :, lanes(j)] + mixing_rate * (
            total - out_estimate[0, :, lanes(j)]
        )

    def guarded(run, j, count):
        @pl.when(jnp.logical_and(j >= 0, j < count))
        def _():
            run(j)

    multiply(0, lambda: pl.semaphore_wait(barrier, 6))
    multiply(1, lambda: None)

    def body(t, carry):
        guarded(lambda i: pair_copy(i).wait_recv(), t, items)
        for way in (0, 1):
            pass_on(way, t)
        guarded(compress, t - first, chunks)
        guarded(forward, t - first - LAG, chunks)
        guarded(finish, t - first - 2 * LAG, chunks)
        guarded(lambda i: multiply(i, lambda: None), t + 2, items)
        return carry

    lax.fori_loop(0, slots + LAG * (chips + 1), body, 0)

    def drain_pair(i, carry):
        pair_copy(i).wait_send()
        return carry

    def drain_line(slot, carry):
        for way in (0, 1):
            count = (chips - 1 - place[way]) * chunks

            @pl.when(jnp.logical_and(slot < count, slot >= count - DEPTH))
            def _(way=way):
                line_copy(way, slot).wait_send()
        return carry

    def drain(j, carry):
        near_copy(j).wait_send()
        far_copy(j).wait_send()
        return carry

    lax.fori_loop(0, items, drain_pair, 0)
    lax.fori_loop(0, slots, drain_line, 0)
    lax.fori_loop(0, chunks, drain, 0)


def on_device(members, groups, params, estimate, mixed, acts, grads, exponents, edges):
    rows, width = params.shape[1:]
    tokens = acts.shape[0]
    chunks = CHUNKS
    cols = width // chunks
    chips = members // 2
    items = chips // 2 * chunks
    slots = (chips - 1) * chunks
    factor = step_size / math.sqrt(members * tokens)
    cfg = (members, groups, chunks, rows, width, tokens, factor)
    wide = (chunks, rows, cols)
    tall = (items, 2, rows, cols)
    dma = pltpu.SemaphoreType.DMA
    any_spec = pl.BlockSpec(memory_space=pl.ANY)
    smem = pl.BlockSpec(memory_space=pltpu.SMEM)
    return pl.pallas_call(
        functools.partial(kernel, cfg),
        out_shape=[pltpu.VMEM(params.shape, f32)] * 3,
        in_specs=[any_spec] * 5 + [smem] * 2,
        out_specs=[pl.BlockSpec(memory_space=pltpu.VMEM)] * 3,
        scratch_shapes=[
            pltpu.VMEM((members, tokens, rows), bf16),
            pltpu.VMEM((members, rows, tokens), bf16),
            pltpu.VMEM((chunks, tokens, cols), bf16),
            *[pltpu.VMEM(wide, f32)] * 3,
            *[pltpu.VMEM(tall, bf16)] * 3,
            pltpu.VMEM((2, slots, rows, cols), bf16),
            pltpu.VMEM((2, slots + chunks, rows, cols), bf16),
            *[pltpu.VMEM(wide, bf16)] * 3,
            dma((members,)), dma((chunks,)), dma((chunks,)), dma((chunks,)), dma((chunks,)),
            dma((items,)), dma((items,)), dma((2, slots)), dma((2, slots)),
            dma((chunks,)), dma((chunks,)), dma((chunks,)), dma((chunks,)),
        ],
        compiler_params=pltpu.CompilerParams(
            collective_id=0, has_side_effects=True, vmem_limit_bytes=53 * 1024 * 1024
        ),
    )(params, estimate, mixed, acts, grads, exponents, edges)


def solution(mesh):
    shard = P("grp", "mem", None)
    tokens = P(("grp", "mem"), None)
    return jax.shard_map(
        functools.partial(on_device, mesh.shape["mem"], mesh.shape["grp"]),
        mesh=mesh,
        in_specs=(shard, shard, shard, tokens, tokens, P("grp", "mem"), P()),
        out_specs=(shard, shard, shard),
        check_vma=False,
    )
```

time: 99.2 us -> 93.1 us (0.939); the launches traced: 97.5 us -> 93 us
  local copies, waits for them, and re-layouts: 6.95 us -> 3.96 us
  Pallas kernels: 89.9 us -> 88.4 us
    unnamed x7 -> x3, local copies, waits for them, and re-layouts: 6.95 us -> 3.96 us
    pallas_call x1, Pallas kernels: 89.9 us -> 88.4 us  [on_device(): pl.pallas_call(functools.partial(kernel, cfg), out_shape=[pltpu.VMEM(para...]
where the time goes in v2:
time: 93.1 us; the launch traced here: 93 us
  Pallas kernels  88.4 us (95%)
  local copies, waits for them, and re-layouts  3.96 us (4%)
    pallas_call x1, Pallas kernels, on_device(): pl.pallas_call(functools.partial(kernel, cfg), out_shape=[pltpu.VMEM(para...  88.4 us
    unnamed x3, local copies, waits for them, and re-layouts  3.96 us

profile of v2, /device:TPU:8, one launch (start us, length us, event | category | flops | bytes accessed | tf_op | source)
XLA Modules:
  0.0 93.0 jit_solution(16656973109615071791)
XLA Ops:
  0.6 88.4 %shard_map.94 = (f32[1,256,2048]{2,1,0:T(8,128)S(1)}, f32[1,256,2048]{2,1,0:T(8,128)S(1)}, f32[1,256,2048]{2,1,0:T(8,128)S(1)}) custom-call(f32[1,256,2048]{2,1,0:T(8,128)} %params.1, f32[1,256,2048]{2,1,0:T(8,128)} %estimate.1, f32[1,256,2048]{2,1,0:T(8,128)} %mixed.1, bf16[1024,2048]{1,0:T(8,128)(2,1)} %acts.1, bf16[1024,2048]{1,0:T(8,128)(2,1)} %grads.1, ...), custom_call_target="tpu_custom_call" | custom-call | tf_op jit(solution)/shard_map/pallas_call | solution.py:306
  89.0 1.3 %copy.13 = f32[1,256,2048]{2,1,0:T(8,128)} copy(f32[1,256,2048]{2,1,0:T(8,128)S(1)} %get-tuple-element.3) | data formatting | bytes 4194304
  90.3 1.3 %copy.14 = f32[1,256,2048]{2,1,0:T(8,128)} copy(f32[1,256,2048]{2,1,0:T(8,128)S(1)} %get-tuple-element.4) | data formatting | bytes 4194304
  91.6 1.3 %copy.15 = f32[1,256,2048]{2,1,0:T(8,128)} copy(f32[1,256,2048]{2,1,0:T(8,128)S(1)} %get-tuple-element.5) | data formatting | bytes 4194304
